TPU v7x, 32 devices: a whole 2x2x4 slice. The times are simulated.
32 devices in a mesh: ctx: 4 (over y, x), fsdp: 8 (over z, core).
Axes of the slice: x: 2, y: 2, z: 4, core: 2. Of those that a mesh axis runs over, the one named last changes fastest.
Arguments:
- layer_input: bfloat16 [1280, 4, 1536], P(('ctx', 'fsdp')), may hold values from -6 to 6
- block_order: int32 [2, 8], replicated, may hold values from 0 to 7, each once within a row
- first_gain: bfloat16 [1536], P('fsdp'), may hold values from 0.25 to 1.75
- w_qkv: bfloat16 [1536, 2048], P('fsdp'), may hold values from -0.15625 to 0.15625
- b_qkv: bfloat16 [2048], P('fsdp'), may hold values from -1.5 to 1.5
- w_o: bfloat16 [1536, 1536], P('fsdp'), may hold values from -1.25 to 1.25
- second_gain: bfloat16 [1536], P('fsdp'), may hold values from 0.25 to 1.75
- w_gate: bfloat16 [1536, 8960], P('fsdp'), may hold values from -0.15625 to 0.15625
- w_up: bfloat16 [1536, 8960], P('fsdp'), may hold values from -0.15625 to 0.15625
- w_down: bfloat16 [8960, 1536], P('fsdp'), may hold values from -0.0625 to 0.0625
- cotangent: bfloat16 [1280, 4, 1536], P(('ctx', 'fsdp')), may hold values from -6 to 6
Outputs:
- mixed: bfloat16 [1280, 4, 1536], P(('ctx', 'fsdp'))
- input_grad: float32 [1280, 4, 1536], P(('ctx', 'fsdp'))
- first_gain_grad: float32 [1536], P('fsdp')
- w_qkv_grad: float32 [1536, 2048], P('fsdp')
- b_qkv_grad: float32 [1792], P('fsdp')
- value_bias_grad: float32 [256], P('fsdp')
- w_o_grad: float32 [1536, 1536], P('fsdp')
- second_gain_grad: float32 [1536], P('fsdp')
- w_gate_grad: float32 [1536, 8960], P('fsdp')
- w_up_grad: float32 [1536, 8960], P('fsdp')
- w_down_grad: float32 [8960, 1536], P('fsdp')
Inputs may be any that keep to these rules, and one draw needn't show every extreme that they name: `block_order`: each row is a permutation.
All inputs are finite; a program needn't handle non-finite values.
Results may differ from a plain program's by a relative error of at most 0.02.
Values may be sent and summed in bfloat16 or wider, within the bound.
A program may use at most 576 MiB of HBM per device.

v0:
```python
import math
import jax
import jax.numpy as jnp
from jax import lax
from jax.sharding import PartitionSpec as P

D = 1536
H = 12
KVH = 2
HD = 128
FF = 8960
SEQS = 2
QKV = 2048
QK = 1792
EPS = 1e-06
THETA = 1000000.0
KEY_BLOCK = 256
NEG_FILL = -1e30
CONTRACT_LAST = (((1,), (1,)), ((), ()))
CONTRACT_FIRST = (((0,), (0,)), ((), ()))


def narrowed(values):
    return lax.optimization_barrier(values.astype(jnp.bfloat16)).astype(jnp.float32)


def block_positions(block_order, first_row, row_count, block_rows, ctx_size):
    row_index = first_row + jnp.arange(row_count, dtype=jnp.int32)
    slot_index = jnp.arange(2 * SEQS, dtype=jnp.int32)
    entries = (slot_index // SEQS)[None, :] * ctx_size + (row_index // block_rows)[:, None]
    tiled = jnp.tile(block_order, (2, 1))
    entry_ids = jnp.arange(2 * ctx_size, dtype=jnp.int32)
    picked = jnp.sum(
        jnp.where(entries[:, :, None] == entry_ids[None, None, :], tiled[None, :, :], 0), -1
    )
    return picked * block_rows + (row_index % block_rows)[:, None]


def pos_groups(positions):
    row_count = positions.shape[0]
    return positions.reshape(row_count, 2, SEQS).transpose(2, 0, 1).reshape(SEQS, row_count * 2)


def to_groups(tokens, row_count, group_size):
    shaped = tokens.reshape(row_count, 2, SEQS, KVH, group_size, HD)
    return shaped.transpose(2, 3, 4, 0, 1, 5).reshape(SEQS, KVH, group_size * row_count * 2, HD)


def from_groups(grouped, row_count, group_size):
    shaped = grouped.reshape(SEQS, KVH, group_size, row_count, 2, HD).transpose(3, 4, 0, 1, 2, 5)
    return shaped.reshape(row_count * 2 * SEQS, KVH * group_size * HD)


def rope_tables(positions):
    half_width = HD // 2
    frequency = THETA ** (-jnp.arange(half_width, dtype=jnp.float32) * 2.0 / HD)
    angles = positions.astype(jnp.float32)[:, None] * frequency[None, :]
    cosine_table = jnp.concatenate([jnp.cos(angles), jnp.cos(angles)], -1)[:, None, :]
    sine_table = jnp.concatenate([jnp.sin(angles), jnp.sin(angles)], -1)[:, None, :]
    return (cosine_table, sine_table)


def rotate(head_values, cosine_table, sine_table):
    half_width = HD // 2
    turned = jnp.concatenate([-head_values[..., half_width:], head_values[..., :half_width]], -1)
    return head_values * cosine_table + turned * sine_table


def rotate_back(grad_values, cosine_table, sine_table):
    half_width = HD // 2
    moved = grad_values * sine_table
    return grad_values * cosine_table + jnp.concatenate(
        [moved[..., half_width:], -moved[..., :half_width]], -1
    )


def normalize(values, gain):
    scale = lax.rsqrt(jnp.mean(values * values, -1, keepdims=True) + EPS)
    unit = values * scale
    return (unit, scale, unit * gain)


def norm_back(grad_out, unit, scale, gain):
    grad_unit = grad_out * gain
    inner = jnp.mean(grad_unit * unit, -1, keepdims=True)
    return (scale * (grad_unit - unit * inner), jnp.sum(grad_out * unit, 0))


def split_blocks(piece):
    row_count = piece.shape[0]
    size = math.gcd(row_count, KEY_BLOCK)
    stacked = piece.reshape(row_count // size, size, piece.shape[1], piece.shape[2])
    firsts = size * jnp.arange(row_count // size, dtype=jnp.int32)
    return (stacked, firsts)


def shards(
    layer_input,
    block_order,
    first_gain,
    w_qkv,
    b_qkv,
    w_o,
    second_gain,
    w_gate,
    w_up,
    w_down,
    cotangent,
):
    ctx_size = lax.axis_size("ctx")
    shard_count = lax.axis_size("fsdp")
    rows_here = layer_input.shape[0]
    slots = layer_input.shape[1]
    block_rows = rows_here * shard_count
    group_size = H // KVH
    kv_width = KVH * HD
    first_row = (lax.axis_index("ctx") * shard_count + lax.axis_index("fsdp")) * rows_here
    own_pos = block_positions(block_order, first_row, rows_here, block_rows, ctx_size)
    cosine_table, sine_table = rope_tables(own_pos.reshape(-1))
    query_scale = HD ** (-0.5)
    w_qkv_all, w_o_all, bias_all, gain_one, gain_two = (
        lax.all_gather(w_qkv, "fsdp", axis=0, tiled=True),
        lax.all_gather(w_o, "fsdp", axis=0, tiled=True),
        lax.all_gather(b_qkv, "fsdp", axis=0, tiled=True),
        lax.all_gather(first_gain, "fsdp", axis=0, tiled=True),
        lax.all_gather(second_gain, "fsdp", axis=0, tiled=True),
    )
    gain_one = gain_one.astype(jnp.float32)
    gain_two = gain_two.astype(jnp.float32)
    inputs = layer_input.reshape(-1, D).astype(jnp.float32)
    unit_one, scale_one, normed = normalize(inputs, gain_one)
    normed_one = normed.astype(jnp.bfloat16)
    projected = jnp.dot(
        normed_one, w_qkv_all, preferred_element_type=jnp.float32
    ) + bias_all.astype(jnp.float32)
    query_raw = projected[:, : H * HD].reshape(-1, H, HD)
    key_raw = projected[:, H * HD : H * HD + kv_width].reshape(-1, KVH, HD)
    value_raw = projected[:, H * HD + kv_width :]
    query_tokens = (
        (rotate(query_raw, cosine_table, sine_table) * query_scale)
        .astype(jnp.bfloat16)
        .reshape(-1, H * HD)
    )
    key_tokens = (
        rotate(key_raw, cosine_table, sine_table).astype(jnp.bfloat16).reshape(-1, kv_width)
    )
    own_kv = jnp.concatenate([key_tokens, value_raw.astype(jnp.bfloat16)], -1).reshape(
        rows_here, slots, 2 * kv_width
    )
    block_kv = lax.all_gather(own_kv, "fsdp", axis=0, tiled=True)
    queries = to_groups(query_tokens, rows_here, group_size)
    query_pos = jnp.tile(pos_groups(own_pos), (1, group_size))
    query_count = queries.shape[2]

    def piece_keys(key_rows, row_start):
        row_count = key_rows.shape[0]
        flat = key_rows.reshape(row_count * slots, 2 * kv_width)
        keys_grouped = to_groups(flat[:, :kv_width], row_count, 1)
        values_grouped = to_groups(flat[:, kv_width:], row_count, 1)
        key_pos = pos_groups(
            block_positions(block_order, row_start, row_count, block_rows, ctx_size)
        )
        visible = query_pos[:, None, :, None] >= key_pos[:, None, None, :]
        scores = jnp.einsum(
            "snmd,snkd->snmk", queries, keys_grouped, preferred_element_type=jnp.float32
        )
        return (keys_grouped, values_grouped, visible, scores)

    start_state = (
        jnp.full((SEQS, KVH, query_count), NEG_FILL, jnp.float32),
        jnp.zeros((SEQS, KVH, query_count), jnp.float32),
        jnp.zeros((SEQS, KVH, query_count, HD), jnp.float32),
    )
    state = start_state
    stacked, firsts = split_blocks(lax.all_gather(block_kv, "ctx", axis=0, tiled=True))

    def forward_one_block(carry, item):
        best, totals, accum = carry
        key_rows, row_start = item
        keys_grouped, values_grouped, visible, scores = piece_keys(key_rows, row_start)
        scores = jnp.where(visible, scores, NEG_FILL)
        fresh = jnp.maximum(best, jnp.max(scores, -1))
        weights = jnp.where(visible, jnp.exp(scores - fresh[..., None]), 0.0)
        decay = jnp.exp(best - fresh)
        totals = totals * decay + jnp.sum(weights, -1)
        accum = accum * decay[..., None] + jnp.einsum(
            "snmk,snkd->snmd",
            weights.astype(jnp.bfloat16),
            values_grouped,
            preferred_element_type=jnp.float32,
        )
        return ((fresh, totals, accum), None)

    state, unused = lax.scan(forward_one_block, state, (stacked, firsts))
    best, totals, accum = state
    attended_grouped = accum / totals[..., None]
    logsum = best + jnp.log(totals)
    attended_low = from_groups(attended_grouped, rows_here, group_size).astype(jnp.bfloat16)
    middle = inputs + jnp.dot(attended_low, w_o_all, preferred_element_type=jnp.float32)
    unit_two, scale_two, normed = normalize(middle, gain_two)
    normed_two = normed.astype(jnp.bfloat16)
    gate_all, up_all, down_all = (
        lax.all_gather(w_gate, "fsdp", axis=0, tiled=True),
        lax.all_gather(w_up, "fsdp", axis=0, tiled=True),
        lax.all_gather(w_down, "fsdp", axis=0, tiled=True),
    )
    gate_part = jnp.dot(normed_two, gate_all, preferred_element_type=jnp.float32)
    up_part = jnp.dot(normed_two, up_all, preferred_element_type=jnp.float32)
    activated = jax.nn.silu(gate_part)
    hidden = (activated * up_part).astype(jnp.bfloat16)
    mixed_out = middle + jnp.dot(hidden, down_all, preferred_element_type=jnp.float32)
    output = mixed_out.astype(jnp.bfloat16).reshape(rows_here, slots, D)
    gate_all, up_all, down_all = (
        lax.all_gather(w_gate, "fsdp", axis=0, tiled=True),
        lax.all_gather(w_up, "fsdp", axis=0, tiled=True),
        lax.all_gather(w_down, "fsdp", axis=0, tiled=True),
    )
    w_qkv_all, w_o_all = (
        lax.all_gather(w_qkv, "fsdp", axis=0, tiled=True),
        lax.all_gather(w_o, "fsdp", axis=0, tiled=True),
    )
    grad_branch_two = cotangent.reshape(-1, D)
    grad_hidden = lax.dot_general(
        grad_branch_two, down_all, CONTRACT_LAST, preferred_element_type=jnp.float32
    )
    sigmoid_gate = jax.nn.sigmoid(gate_part)
    grad_gate = grad_hidden * up_part * sigmoid_gate * (1.0 + gate_part * (1.0 - sigmoid_gate))
    grad_gate_up = jnp.concatenate([grad_gate, grad_hidden * activated], -1).astype(jnp.bfloat16)
    grad_normed_two = lax.dot_general(
        grad_gate_up[:, :FF], gate_all, CONTRACT_LAST, preferred_element_type=jnp.float32
    )
    grad_normed_two = grad_normed_two + lax.dot_general(
        grad_gate_up[:, FF:], up_all, CONTRACT_LAST, preferred_element_type=jnp.float32
    )
    grad_middle_norm, grad_gain_two = norm_back(grad_normed_two, unit_two, scale_two, gain_two)
    grad_middle = cotangent.reshape(-1, D).astype(jnp.float32) + grad_middle_norm
    grad_branch_one = grad_middle.astype(jnp.bfloat16)
    grad_attended = lax.dot_general(
        grad_branch_one, w_o_all, CONTRACT_LAST, preferred_element_type=jnp.float32
    ).astype(jnp.bfloat16)
    grad_out_grouped = to_groups(grad_attended, rows_here, group_size)
    delta = jnp.sum(grad_out_grouped.astype(jnp.float32) * attended_grouped, -1)
    back_state = (
        jnp.zeros((SEQS, KVH, query_count, HD), jnp.float32),
        jnp.zeros((ctx_size * block_rows, slots, 2 * kv_width), jnp.float32),
    )
    state = back_state
    stacked, firsts = split_blocks(lax.all_gather(block_kv, "ctx", axis=0, tiled=True))

    def backward_one_block(carry, item):
        grad_queries, grad_kv_full = carry
        key_rows, row_start = item
        row_count = key_rows.shape[0]
        keys_grouped, values_grouped, visible, scores = piece_keys(key_rows, row_start)
        probs = jnp.where(
            visible, jnp.exp(jnp.where(visible, scores, NEG_FILL) - logsum[..., None]), 0.0
        )
        grad_probs = jnp.einsum(
            "snmd,snkd->snmk", grad_out_grouped, values_grouped, preferred_element_type=jnp.float32
        )
        grad_scores = (probs * (grad_probs - delta[..., None])).astype(jnp.bfloat16)
        grad_queries = grad_queries + jnp.einsum(
            "snmk,snkd->snmd", grad_scores, keys_grouped, preferred_element_type=jnp.float32
        )
        grad_keys = jnp.einsum(
            "snmk,snmd->snkd", grad_scores, queries, preferred_element_type=jnp.float32
        )
        grad_values = jnp.einsum(
            "snmk,snmd->snkd",
            probs.astype(jnp.bfloat16),
            grad_out_grouped,
            preferred_element_type=jnp.float32,
        )
        block_terms = jnp.concatenate(
            [from_groups(grad_keys, row_count, 1), from_groups(grad_values, row_count, 1)], -1
        ).reshape(row_count, slots, 2 * kv_width)
        previous = lax.dynamic_slice_in_dim(grad_kv_full, row_start, row_count, 0)
        grad_kv_full = lax.dynamic_update_slice_in_dim(
            grad_kv_full, previous + block_terms, row_start, 0
        )
        return ((grad_queries, grad_kv_full), None)

    state, unused = lax.scan(backward_one_block, state, (stacked, firsts))
    grad_queries, grad_kv_full = state
    grad_kv = lax.psum_scatter(grad_kv_full, ("ctx", "fsdp"), scatter_dimension=0, tiled=True)
    grad_kv_low = narrowed(grad_kv).reshape(-1, 2 * kv_width)
    grad_query_tokens = from_groups(narrowed(grad_queries), rows_here, group_size) * query_scale
    grad_query_raw = rotate_back(
        grad_query_tokens.reshape(-1, H, HD), cosine_table, sine_table
    ).reshape(-1, H * HD)
    grad_key_raw = rotate_back(
        grad_kv_low[:, :kv_width].reshape(-1, KVH, HD), cosine_table, sine_table
    ).reshape(-1, kv_width)
    grad_projected = jnp.concatenate(
        [grad_query_raw, grad_key_raw, grad_kv_low[:, kv_width:]], -1
    ).astype(jnp.bfloat16)
    grad_bias = jnp.sum(grad_projected, 0, dtype=jnp.float32)
    grad_bias_qk = grad_bias[:QK]
    grad_bias_value = grad_bias[QK:]
    grad_normed_one = lax.dot_general(
        grad_projected, w_qkv_all, CONTRACT_LAST, preferred_element_type=jnp.float32
    )
    grad_input_norm, grad_gain_one = norm_back(grad_normed_one, unit_one, scale_one, gain_one)
    grad_input = (grad_middle + grad_input_norm).reshape(rows_here, slots, D)
    weight_rows = lax.psum_scatter(
        jnp.concatenate(
            [
                lax.dot_general(
                    normed_two, grad_gate_up, CONTRACT_FIRST, preferred_element_type=jnp.float32
                ),
                lax.dot_general(
                    normed_one, grad_projected, CONTRACT_FIRST, preferred_element_type=jnp.float32
                ),
                lax.dot_general(
                    attended_low,
                    grad_branch_one,
                    CONTRACT_FIRST,
                    preferred_element_type=jnp.float32,
                ),
            ],
            1,
        ).astype(jnp.bfloat16),
        "fsdp",
        scatter_dimension=0,
        tiled=True,
    ).astype(jnp.float32)
    down_rows = lax.psum_scatter(
        lax.dot_general(
            hidden, grad_branch_two, CONTRACT_FIRST, preferred_element_type=jnp.float32
        ).astype(jnp.bfloat16),
        "fsdp",
        scatter_dimension=0,
        tiled=True,
    ).astype(jnp.float32)
    gain_one_rows, gain_two_rows, bias_rows, value_bias_rows = (
        lax.psum_scatter(grad_gain_one, "fsdp", scatter_dimension=0, tiled=True),
        lax.psum_scatter(grad_gain_two, "fsdp", scatter_dimension=0, tiled=True),
        lax.psum_scatter(grad_bias_qk, "fsdp", scatter_dimension=0, tiled=True),
        lax.psum_scatter(grad_bias_value, "fsdp", scatter_dimension=0, tiled=True),
    )
    weight_rows, down_rows, gain_one_rows, gain_two_rows, bias_rows, value_bias_rows = (
        lax.psum(weight_rows.astype(jnp.bfloat16), "ctx").astype(jnp.float32),
        lax.psum(down_rows.astype(jnp.bfloat16), "ctx").astype(jnp.float32),
        lax.psum(gain_one_rows.astype(jnp.bfloat16), "ctx").astype(jnp.float32),
        lax.psum(gain_two_rows.astype(jnp.bfloat16), "ctx").astype(jnp.float32),
        lax.psum(bias_rows.astype(jnp.bfloat16), "ctx").astype(jnp.float32),
        lax.psum(value_bias_rows.astype(jnp.bfloat16), "ctx").astype(jnp.float32),
    )
    return (
        output,
        grad_input,
        gain_one_rows,
        weight_rows[:, 2 * FF : 2 * FF + QKV],
        bias_rows,
        value_bias_rows,
        weight_rows[:, 2 * FF + QKV :],
        gain_two_rows,
        weight_rows[:, :FF],
        weight_rows[:, FF : 2 * FF],
        down_rows,
    )


def solution(mesh):
    in_specs = (
        P(("ctx", "fsdp"), None, None),
        P(),
        P("fsdp"),
        P("fsdp", None),
        P("fsdp"),
        P("fsdp", None),
        P("fsdp"),
        P("fsdp", None),
        P("fsdp", None),
        P("fsdp", None),
        P(("ctx", "fsdp"), None, None),
    )
    out_specs = (
        P(("ctx", "fsdp"), None, None),
        P(("ctx", "fsdp"), None, None),
        P("fsdp"),
        P("fsdp", None),
        P("fsdp"),
        P("fsdp"),
        P("fsdp", None),
        P("fsdp"),
        P("fsdp", None),
        P("fsdp", None),
        P("fsdp", None),
    )
    return jax.shard_map(shards, mesh=mesh, in_specs=in_specs, out_specs=out_specs, check_vma=False)
```

profile of v0, /device:TPU:0, one launch (start us, length us, event | category | flops | bytes accessed | tf_op | source)
XLA Modules:
  0.0 2331.6 jit_solution(8139246037101609936)
XLA Ops:
  9.8 13.5 all-gather
  27.0 15.6 all-reduce.8
  46.4 31.2 %all-gather.9.cloned.1.call-done = bf16[1536,2048]{1,0:T(8,128)(2,1)} async-done(((bf16[192,2048]{1,0:T(8,128)(2,1)}), bf16[1536,2048]{1,0:T(8,128)(2,1)}) %all-gather.9.cloned.1.call-update) | async-done | bytes 6291472 | tf_op jit(solution)/shard_map/all_gather | solution.py:122
  77.6 4.0 convolution_add_fusion.4
  84.0 22.2 all-gather.11.cloned.1.call-done
  125.7 43.1 %all-gather.13.cloned.1.call-done = bf16[1280,4,512]{2,1,0:T(4,128)(2,1)} async-done(((bf16[320,4,512]{2,1,0:T(4,128)(2,1)}), bf16[1280,4,512]{2,1,0:T(4,128)(2,1)}) %all-gather.13.cloned.1.call-update) | async-done | bytes 5242896 | tf_op jit(solution)/shard_map/all_gather | solution.py:175
  168.8 82.5 %while.34 = (s32[]{:T(128)}, f32[2,2,480]{2,1,0:T(2,128)S(1)}, f32[2,2,480]{2,1,0:T(2,128)S(1)}, f32[2,2,480,128]{3,2,1,0:T(8,128)}, s32[5]{0:T(128)S(1)}, /*ind...) while((s32[]{:T(128)}, f32[2,2,480]{2,1,0:T(2,128)S(1)}, ...), condition=%wide.region_6.7_spmd.clone, body=%wide.region_2.6_spmd.clone.sunk | while | flops 514415264 | bytes 27955316 | solution.py:194
  176.3 3.8 fusion.144
  180.6 4.4 fusion.146
  196.7 4.7 fusion.146
  213.0 4.7 fusion.146
  229.2 5.5 fusion.146
  246.4 4.7 fusion.146
  257.4 203.6 %all-gather.17.cloned.1.call-done = bf16[1536,8960]{1,0:T(8,128)(2,1)} async-done(((bf16[192,8960]{1,0:T(8,128)(2,1)}), bf16[1536,8960]{1,0:T(8,128)(2,1)}) %all-gather.17.cloned.1.call-update) | async-done | bytes 27525136 | tf_op jit(solution)/shard_map/all_gather | solution.py:203
  461.0 16.3 fusion.69
  477.3 222.6 %all-gather.19.cloned.1.call-done = bf16[1536,8960]{1,0:T(8,128)(2,1)} async-done(((bf16[192,8960]{1,0:T(8,128)(2,1)}), bf16[1536,8960]{1,0:T(8,128)(2,1)}) %all-gather.19.cloned.1.call-update) | async-done | bytes 27525136 | tf_op jit(solution)/shard_map/all_gather | solution.py:204
  699.9 16.4 fusion.70
  716.4 222.6 %all-gather.21.cloned.1.call-done = bf16[8960,1536]{1,0:T(8,128)(2,1)} async-done(((bf16[1120,1536]{1,0:T(8,128)(2,1)}), bf16[8960,1536]{1,0:T(8,128)(2,1)}) %all-gather.21.cloned.1.call-update) | async-done | bytes 27525136 | tf_op jit(solution)/shard_map/all_gather | solution.py:205
  939.0 19.8 multiply_convert_fusion
  958.8 15.2 convolution_convert_fusion.1
  974.0 17.0 fusion.71
  991.0 16.1 multiply_reduce_fusion
  1008.4 4.1 convolution_convert_fusion.4
  1014.9 4.9 broadcast_in_dim.152
  1019.8 165.6 %while.35 = (s32[]{:T(128)}, f32[2,2,480,128]{3,2,1,0:T(8,128)}, f32[1280,4,512]{2,1,0:T(4,128)}, s32[5]{0:T(128)S(1)}, s32[2,8]{1,0:T(2,128)S(1)}, /*index=5*/b...) while((s32[]{:T(128)}, f32[2,2,480,128]{3,2,1,0:T(8,128)}, ...), condition=%wide.region_12.13_spmd.clone, body=%wide.region_10.12_spmd.clone.sunk | while | flops 1270183168 | bytes 55970532 | solution.py:283
  1027.9 4.0 fusion.160
  1035.5 3.8 fusion.161
  1059.9 4.0 fusion.160
  1068.7 3.8 fusion.161
  1093.0 3.9 fusion.160
  1101.8 4.2 fusion.161
  1126.6 3.9 fusion.160
  1135.4 3.9 fusion.161
  1159.9 3.9 fusion.160
  1168.7 3.8 fusion.161
  1181.4 3.7 fusion.163
  1188.1 176.6 %all-reduce.15 = bf16[1280,4,512]{2,1,0:T(4,128)(2,1)} all-reduce(f32[1280,4,512]{2,1,0:T(4,128)} %get-tuple-element.344), channel_id=2, replica_groups=mesh['ctx'=4,'fsdp'=8] {'ctx','fsdp'}, use_global_device_ids=true, to_apply=%region_13.14.clone | all-reduce | flops 2621440 | bytes 15728640
  1376.0 4.6 convolution_convert_fusion.2
  1380.7 23.8 %convolution_convert_fusion = bf16[1536,17920]{1,0:T(8,128)(2,1)} fusion(bf16[160,1536]{1,0:T(8,128)(2,1)S(1)} %copy-done.10, bf16[160,8960]{1,0:T(8,128)(2,1)} %get-tuple-element.485, bf16[160,8960]{1,0:T(8,128)(2,1)} %get-tuple-element.486), kind=kOutput, calls=%fused_computation.72 | convolution fusion | flops 8847032320 | bytes 61276160 | tf_op jit(solution)/shard_map/dot_general | solution.py:308
  1404.5 44.2 %pad_maximum_fusion = bf16[1536,21504]{1,0:T(8,128)(2,1)} fusion(bf16[1536,1536]{1,0:T(8,128)(2,1)} %convolution_convert_fusion.3, bf16[1536,2048]{1,0:T(8,128)(2,1)} %convolution_convert_fusion.2, bf16[1536,17920]{1,0:T(8,128)(2,1)} %convolution_convert_fusion), kind=kLoop, calls=%fused_computation.73 | loop fusion | flops 198180864 | bytes 132120576 | tf_op jit(solution)/shard_map/concatenate | solution.py:306
  1448.8 629.6 %reduce-scatter.3.cloned.1.call-done = bf16[192,21504]{1,0:T(8,128)(2,1)} async-done(((bf16[1536,21504]{1,0:T(8,128)(2,1)}), bf16[192,21504]{1,0:T(8,128)(2,1)}) %reduce-scatter.3.cloned.1.call-update) | async-done | bytes 8257552 | tf_op jit(solution)/shard_map/reduce_scatter | solution.py:305
  2080.4 16.4 fusion.44
  2098.7 5.7 multiply_reduce_fusion.1
  2107.0 26.1 %all-reduce.7 = (bf16[1536]{0:T(1024)(128)(2,1)S(1)}, bf16[1792]{0:T(1024)(128)(2,1)S(1)}, bf16[256]{0:T(256)(128)(2,1)S(1)}, bf16[1536]{0:T(1024)(128)(2,1)S(1)}) all-reduce(f32[1536]{0:T(1024)S(1)} %get-tuple-element.419, f32[1792]{0:T(1024)S(1)} %bitcast.253, ...), channel_id=3, replica_groups=mesh['ctx'=4,'fsdp'=8] {'fsdp'}, use_global_device_ids=true, to_apply=%region_16.17.clone | all-reduce | flops 5120 | bytes 30720
  2133.4 10.2 all-reduce.9
  2145.9 160.7 %all-reduce.14.cloned.1.call-done = (bf16[192,21504]{1,0:T(8,128)(2,1)}, bf16[1120,1536]{1,0:T(8,128)(2,1)}) async-done(((bf16[192,21504]{1,0:T(8,128)(2,1)}, bf16[1120,1536]{1,0:T(8,128)(2,1)}), (bf16[192,21504]{1,0:T(8,128)(2,1)}, bf16[1120,1536]{1,0:T(8,128)(2,1)})) %all-reduce.14.cloned.1.call-update) | async-done | bytes 11698192 | tf_op jit(solution)/shard_map/psum | solution.py:342
  2311.2 9.2 fusion.62
  2320.5 3.9 convert_element_type.184
  (488 shorter events, 231.9 us)
Async XLA Ops:
  7.2 70.4 %all-gather.9.cloned.1.call-start = ((), (), s32[]{:S(2)}) async-start(), calls=%async_computation.2 | async-start | bytes 7077888 | tf_op jit(solution)/shard_map/all_gather | solution.py:122
  7.9 98.2 %all-gather.11.cloned.1.call-start = ((), (), s32[]{:S(2)}) async-start(), calls=%async_computation.3 | async-start | bytes 1474560 | tf_op jit(solution)/shard_map/all_gather | solution.py:150
  9.1 72.6 %copy-start = (f32[160,1536]{1,0:T(8,128)}, f32[160,1536]{1,0:T(8,128)S(1)}, u32[]{:S(2)}) copy-start(f32[160,1536]{1,0:T(8,128)S(1)} %reshape.608) | copy-start | bytes 2949124
  42.6 39.1 %copy-start.29 = (f32[1536]{0:T(1024)}, f32[1536]{0:T(1024)S(1)}, u32[]{:S(2)}) copy-start(f32[1536]{0:T(1024)S(1)} %convert_element_type.151) | copy-start | bytes 18436
  44.1 33.6 %copy-start.32 = (f32[160]{0:T(256)}, f32[160]{0:T(256)S(1)}, u32[]{:S(2)}) copy-start(f32[160]{0:T(256)S(1)} %rsqrt.20) | copy-start | bytes 1924
  45.6 36.7 %copy-start.26 = (f32[160,128]{1,0:T(8,128)}, f32[160,128]{1,0:T(8,128)S(1)}, u32[]{:S(2)}) copy-start(f32[160,128]{1,0:T(8,128)S(1)} %pad_maximum_fusion.4) | copy-start | bytes 245764
  46.4 35.7 %copy-start.24 = (f32[160,128]{1,0:T(8,128)}, f32[160,128]{1,0:T(8,128)S(1)}, u32[]{:S(2)}) copy-start(f32[160,128]{1,0:T(8,128)S(1)} %get-tuple-element.501) | copy-start | bytes 245764
  81.7 25.7 %copy-start.13 = (f32[160,2048]{1,0:T(8,128)}, f32[160,2048]{1,0:T(8,128)S(1)}, u32[]{:S(2)}) copy-start(f32[160,2048]{1,0:T(8,128)S(1)} %convolution_add_fusion.4) | copy-start | bytes 3932164
  83.9 84.9 %all-gather.13.cloned.1.call-start = ((), (), s32[]{:S(2)}) async-start(), calls=%async_computation.4 | async-start | bytes 6553600 | tf_op jit(solution)/shard_map/all_gather | solution.py:175
  106.1 147.5 %all-gather.15.cloned.1.call-start = ((), (), s32[]{:S(2)}) async-start(), calls=%async_computation.5 | async-start | bytes 5308416 | tf_op jit(solution)/shard_map/all_gather | solution.py:123
  106.7 354.3 %all-gather.17.cloned.1.call-start = ((), (), s32[]{:S(2)}) async-start(), calls=%async_computation.6 | async-start | bytes 30965760 | tf_op jit(solution)/shard_map/all_gather | solution.py:203
  107.3 1.9 copy-start.28
  107.3 592.6 %all-gather.19.cloned.1.call-start = ((), (), s32[]{:S(2)}) async-start(), calls=%async_computation.7 | async-start | bytes 30965760 | tf_op jit(solution)/shard_map/all_gather | solution.py:204
  107.4 5.0 copy-start.14
  107.9 831.1 %all-gather.21.cloned.1.call-start = ((), (), s32[]{:S(2)}) async-start(), calls=%async_computation.8 | async-start | bytes 30965760 | tf_op jit(solution)/shard_map/all_gather | solution.py:205
  108.7 1340.1 %reduce-scatter.5.cloned.1.call-start = ((), (), s32[]{:S(2)}) async-start(), calls=%async_computation.10 | async-start | bytes 30965760 | tf_op jit(solution)/shard_map/reduce_scatter | solution.py:327
  116.4 7.4 copy-start.15
  122.0 46.8 %copy-start.31 = (s32[2,8]{1,0:T(2,128)S(1)}, s32[2,8]{1,0:T(2,128)}, u32[]{:S(2)}) copy-start(s32[2,8]{1,0:T(2,128)} %param.16) | copy-start | bytes 196
  251.3 2.4 copy-start.1
  253.7 3.8 copy-start.11
  257.2 749.9 %copy-start.7 = (f32[160,1536]{1,0:T(8,128)}, f32[160,1536]{1,0:T(8,128)S(1)}, u32[]{:S(2)}) copy-start(f32[160,1536]{1,0:T(8,128)S(1)} %get-tuple-element.513) | copy-start | bytes 2949124
  257.4 442.5 %copy-start.9 = (bf16[160,1536]{1,0:T(8,128)(2,1)}, bf16[160,1536]{1,0:T(8,128)(2,1)S(1)}, u32[]{:S(2)}) copy-start(bf16[160,1536]{1,0:T(8,128)(2,1)S(1)} %multiply_convert_fusion.3) | copy-start | bytes 1474564
  477.3 461.7 %copy-start.16 = (bf16[160,1536]{1,0:T(8,128)(2,1)S(1)}, bf16[160,1536]{1,0:T(8,128)(2,1)}, u32[]{:S(2)}) copy-start(bf16[160,1536]{1,0:T(8,128)(2,1)} %reshape.600) | copy-start | bytes 1474564
  974.0 1104.4 %reduce-scatter.3.cloned.1.call-start = ((), (), s32[]{:S(2)}) async-start(), calls=%async_computation.9 | async-start | bytes 74317824 | tf_op jit(solution)/shard_map/reduce_scatter | solution.py:305
  1008.4 5.8 copy-start.17
  1027.9 4.0 copy-start.5
  1031.9 3.6 copy-start.6
  1059.9 4.0 copy-start.5
  1063.8 4.9 copy-start.6
  1093.0 3.9 copy-start.5
  1096.9 4.9 copy-start.6
  1126.6 3.9 copy-start.5
  1130.5 4.9 copy-start.6
  1159.8 3.9 copy-start.5
  1163.8 4.9 copy-start.6
  1365.6 3.5 copy-start.25
  1365.8 3.9 copy-start.22
  1369.2 2.0 copy-start.4
  1369.2 2.0 copy-start.12
  1369.8 5.8 copy-start.23
  1371.2 3.6 copy-start.27
  1371.2 3.7 copy-start.18
  1374.8 1.2 copy-start.33
  1376.0 4.6 copy-start.10
  1448.7 857.9 %all-reduce.14.cloned.1.call-start = ((), (), s32[]{:S(2)}) async-start(), calls=%async_computation.11 | async-start | bytes 23396352 | tf_op jit(solution)/shard_map/psum | solution.py:342
  2078.4 2.1 copy-start.8
  2104.5 2.6 copy-start.34
  2311.2 9.2 copy-start.19
  (5 other events, 4.8 us)
Sparse Core Ops, SparseCore 0:
  9.6 67.9 all-gather.8
  84.0 22.0 all-gather.10
  108.0 60.8 all-gather.12
  170.3 51.1 all-gather.14
  223.1 237.9 all-gather.16
  462.5 237.3 all-gather.18
  701.6 237.3 all-gather.20
  974.1 267.4 reduce-scatter.4
  1448.8 629.5 reduce-scatter.2
  2082.0 224.5 all-reduce.13
where the time goes:
time: 2340 us; the launch traced here: 2330 us
  waiting for transfers between devices  1540 us (66%)
  matrix products  274 us (12%)
  blocking collectives  242 us (10%)
  local copies, waits for them, and re-layouts  128 us (5%)
  other arithmetic  118 us (5%)
    reduce_scatter x1, waiting for transfers between devices, shards(): lax.psum_scatter(jnp.concatenate([lax.dot_general(normed_two, grad_gate_u...  630 us
    all_gather x1, waiting for transfers between devices, shards(): lax.all_gather(w_down, 'fsdp', axis=0, tiled=True)  223 us
    all_gather x1, waiting for transfers between devices, shards(): lax.all_gather(w_up, 'fsdp', axis=0, tiled=True)  223 us
    unnamed x3, blocking collectives  218 us
    all_gather x1, waiting for transfers between devices, shards(): lax.all_gather(w_gate, 'fsdp', axis=0, tiled=True)  204 us
    psum x1, waiting for transfers between devices, shards(): lax.psum(weight_rows.astype(jnp.bfloat16), 'ctx').astype(jnp.float32)  161 us
  transfers between devices with their start and end apart: 10, of which 8 were waited for; matrix products, arithmetic and copies ran while one was open for 20% of the time, Pallas kernels for 0%

commit v1 on v0

--- a/solution.py
+++ b/solution.py
@@ -199,8 +199,26 @@
     middle = inputs + jnp.dot(attended_low, w_o_all, preferred_element_type=jnp.float32)
     unit_two, scale_two, normed = normalize(middle, gain_two)
     normed_two = normed.astype(jnp.bfloat16)
+
+    def pass_levels_all(x0, array_dim):
+        net_axis = "fsdp"
+        a_now = lax.axis_size(net_axis)
+        tall = lax.axis_index(net_axis)
+        mixed_arr, frame_out = (a_now, tall)
+        carry_out, arr_next = (x0, 1)
+        while arr_next < mixed_arr:
+            series = []
+            for tick in range(mixed_arr):
+                series.append((tick, tick ^ arr_next))
+            f_next = lax.ppermute(carry_out, axis_name=net_axis, perm=series)
+            o_now = jnp.concatenate([carry_out, f_next], axis=array_dim)
+            clean = jnp.concatenate([f_next, carry_out], axis=array_dim)
+            carry_out = jnp.where(frame_out & arr_next == 0, o_now, clean)
+            arr_next = 2 * arr_next
+        return carry_out
+
     gate_all, up_all, down_all = (
-        lax.all_gather(w_gate, "fsdp", axis=0, tiled=True),
+        pass_levels_all(w_gate, 0),
         lax.all_gather(w_up, "fsdp", axis=0, tiled=True),
         lax.all_gather(w_down, "fsdp", axis=0, tiled=True),
     )

time: 2340 us -> 2950 us (1.26)
  waiting for transfers between devices: 1540 us -> 2110 us
    ppermute x0 -> x3, waiting for transfers between devices: none -> 671 us  [pass_levels_all(): f_next = lax.ppermute(carry_out, axis_name=net_axis, perm=series)]
    all_gather x1, waiting for transfers between devices: 223 us -> 531 us  [shards(): lax.all_gather(w_up, 'fsdp', axis=0, tiled=True)]
    all_gather x1, waiting for transfers between devices: 204 us -> 0.02 us  [shards(): lax.all_gather(w_gate, 'fsdp', axis=0, tiled=True)]
    all_gather x1, waiting for transfers between devices: 223 us -> 64.7 us  [shards(): lax.all_gather(w_down, 'fsdp', axis=0, tiled=True)]
    all_gather x1, waiting for transfers between devices: 43.1 us -> 0.02 us  [shards(): lax.all_gather(block_kv, 'ctx', axis=0, tiled=True)]
  transfers between devices with their start and end apart: 10 -> 13, of which waited for: 8 -> 9; matrix products, arithmetic and copies ran while one was open for 20% -> 18% of each run, Pallas kernels for 0% -> 0%
where the time goes in v1:
time: 2950 us; the launch traced here: 2940 us
  waiting for transfers between devices  2110 us (72%)
  matrix products  279 us (9%)
  blocking collectives  241 us (8%)
  other arithmetic  143 us (5%)
  local copies, waits for them, and re-layouts  130 us (4%)
    ppermute x3, waiting for transfers between devices, pass_levels_all(): f_next = lax.ppermute(carry_out, axis_name=net_axis, perm=series)  671 us
    reduce_scatter x1, waiting for transfers between devices, shards(): lax.psum_scatter(jnp.concatenate([lax.dot_general(normed_two, grad_gate_u...  629 us
    all_gather x1, waiting for transfers between devices, shards(): lax.all_gather(w_up, 'fsdp', axis=0, tiled=True)  531 us
    unnamed x3, blocking collectives  218 us
    psum x1, waiting for transfers between devices, shards(): lax.psum(weight_rows.astype(jnp.bfloat16), 'ctx').astype(jnp.float32)  161 us
    all_gather x1, waiting for transfers between devices, shards(): lax.all_gather(w_down, 'fsdp', axis=0, tiled=True)  64.7 us
  transfers between devices with their start and end apart: 13, of which 9 were waited for; matrix products, arithmetic and copies ran while one was open for 18% of the time, Pallas kernels for 0%

profile of v1, /device:TPU:0, one launch (start us, length us, event | category | flops | bytes accessed | tf_op | source)
XLA Modules:
  0.0 2938.9 jit_solution(7707366536420569723)
XLA Ops:
  9.8 13.5 all-gather
  27.0 15.6 all-reduce.8
  46.4 31.2 %all-gather.9.cloned.1.call-done = bf16[1536,2048]{1,0:T(8,128)(2,1)} async-done(((bf16[192,2048]{1,0:T(8,128)(2,1)}), bf16[1536,2048]{1,0:T(8,128)(2,1)}) %all-gather.9.cloned.1.call-update) | async-done | bytes 6291472 | tf_op jit(solution)/shard_map/all_gather | solution.py:122
  77.6 4.0 convolution_add_fusion.4
  84.0 22.2 all-gather.11.cloned.1.call-done
  109.0 6.0 collective-permute-done
  115.0 7.3 maximum_select_fusion.3
  127.9 304.0 %collective-permute-done.1 = bf16[384,8960]{1,0:T(8,128)(2,1)} collective-permute-done((bf16[384,8960]{1,0:T(8,128)(2,1)}, bf16[384,8960]{1,0:T(8,128)(2,1)}, u32[]{:S(2)}, u32[]{:S(2)}) %collective-permute-start.1) | collective-permute-done | bytes 6881312 | tf_op jit(solution)/shard_map/ppermute | solution.py:213
  431.8 16.4 maximum_select_fusion.2
  461.3 81.3 %while.34 = (s32[]{:T(128)}, f32[2,2,480]{2,1,0:T(2,128)S(1)}, f32[2,2,480]{2,1,0:T(2,128)S(1)}, f32[2,2,480,128]{3,2,1,0:T(8,128)}, s32[5]{0:T(128)S(1)}, /*ind...) while((s32[]{:T(128)}, f32[2,2,480]{2,1,0:T(2,128)S(1)}, ...), condition=%wide.region_6.7_spmd.clone, body=%wide.region_2.6_spmd.clone.sunk | while | flops 514415264 | bytes 27955316 | solution.py:194
  473.1 4.4 fusion.153
  489.1 4.8 fusion.153
  505.4 4.7 fusion.153
  521.6 4.7 fusion.153
  537.8 4.7 fusion.153
  548.9 64.7 %all-gather.19.cloned.1.call-done = bf16[8960,1536]{1,0:T(8,128)(2,1)} async-done(((bf16[1120,1536]{1,0:T(8,128)(2,1)}), bf16[8960,1536]{1,0:T(8,128)(2,1)}) %all-gather.19.cloned.1.call-update) | async-done | bytes 27525136 | tf_op jit(solution)/shard_map/all_gather | solution.py:223
  613.6 17.1 fusion.78
  630.7 531.1 %all-gather.17.cloned.1.call-done = bf16[1536,8960]{1,0:T(8,128)(2,1)} async-done(((bf16[192,8960]{1,0:T(8,128)(2,1)}), bf16[1536,8960]{1,0:T(8,128)(2,1)}) %all-gather.17.cloned.1.call-update) | async-done | bytes 27525136 | tf_op jit(solution)/shard_map/all_gather | solution.py:222
  1161.8 15.6 fusion.77
  1177.3 360.9 %collective-permute-done.2 = bf16[768,8960]{1,0:T(8,128)(2,1)} collective-permute-done((bf16[768,8960]{1,0:T(8,128)(2,1)}, bf16[768,8960]{1,0:T(8,128)(2,1)}, u32[]{:S(2)}, u32[]{:S(2)}) %collective-permute-start.2) | collective-permute-done | bytes 13762592 | tf_op jit(solution)/shard_map/ppermute | solution.py:213
  1538.2 26.3 multiply_convert_fusion
  1564.5 14.7 convolution_convert_fusion.1
  1579.4 16.3 fusion.79
  1595.7 16.1 multiply_reduce_fusion
  1613.1 4.2 convolution_convert_fusion.4
  1619.6 4.9 broadcast_in_dim.152
  1624.5 165.9 %while.35 = (s32[]{:T(128)}, f32[2,2,480,128]{3,2,1,0:T(8,128)}, f32[1280,4,512]{2,1,0:T(4,128)}, s32[5]{0:T(128)S(1)}, s32[2,8]{1,0:T(2,128)S(1)}, /*index=5*/b...) while((s32[]{:T(128)}, f32[2,2,480,128]{3,2,1,0:T(8,128)}, ...), condition=%wide.region_12.13_spmd.clone, body=%wide.region_10.12_spmd.clone.sunk | while | flops 1270183168 | bytes 54004424 | solution.py:301
  1632.6 3.9 fusion.167
  1640.1 4.1 fusion.168
  1664.7 3.9 fusion.167
  1673.4 4.0 fusion.168
  1698.0 3.9 fusion.167
  1706.7 3.9 fusion.168
  1731.3 4.0 fusion.167
  1740.1 3.9 fusion.168
  1764.6 4.0 fusion.167
  1773.5 4.1 fusion.168
  1793.1 176.1 %all-reduce.15 = bf16[1280,4,512]{2,1,0:T(4,128)(2,1)} all-reduce(f32[1280,4,512]{2,1,0:T(4,128)} %get-tuple-element.344), channel_id=2, replica_groups=mesh['ctx'=4,'fsdp'=8] {'ctx','fsdp'}, use_global_device_ids=true, to_apply=%region_13.14.clone | all-reduce | flops 2621440 | bytes 15728640
  1983.7 4.6 convolution_convert_fusion.2
  1988.3 23.8 convolution_convert_fusion
  2012.1 44.2 %pad_maximum_fusion = bf16[1536,21504]{1,0:T(8,128)(2,1)} fusion(bf16[1536,1536]{1,0:T(8,128)(2,1)} %convolution_convert_fusion.3, bf16[1536,2048]{1,0:T(8,128)(2,1)} %convolution_convert_fusion.2, bf16[1536,17920]{1,0:T(8,128)(2,1)} %convolution_convert_fusion), kind=kLoop, calls=%fused_computation.73 | loop fusion | flops 198180864 | bytes 132120576 | tf_op jit(solution)/shard_map/concatenate | solution.py:324
  2056.4 629.3 %reduce-scatter.3.cloned.1.call-done = bf16[192,21504]{1,0:T(8,128)(2,1)} async-done(((bf16[1536,21504]{1,0:T(8,128)(2,1)}), bf16[192,21504]{1,0:T(8,128)(2,1)}) %reduce-scatter.3.cloned.1.call-update) | async-done | bytes 8257552 | tf_op jit(solution)/shard_map/reduce_scatter | solution.py:323
  2687.7 16.4 fusion.51
  2706.0 5.7 multiply_reduce_fusion.1
  2714.4 26.1 all-reduce.7
  2740.7 10.2 all-reduce.9
  2753.2 160.7 %all-reduce.14.cloned.1.call-done = (bf16[192,21504]{1,0:T(8,128)(2,1)}, bf16[1120,1536]{1,0:T(8,128)(2,1)}) async-done(((bf16[192,21504]{1,0:T(8,128)(2,1)}, bf16[1120,1536]{1,0:T(8,128)(2,1)}), (bf16[192,21504]{1,0:T(8,128)(2,1)}, bf16[1120,1536]{1,0:T(8,128)(2,1)})) %all-reduce.14.cloned.1.call-update) | async-done | bytes 11698192 | tf_op jit(solution)/shard_map/psum | solution.py:360
  2918.5 9.2 fusion.70
  (484 shorter events, 247.6 us)
Async XLA Ops:
  7.2 70.4 %all-gather.9.cloned.1.call-start = ((), (), s32[]{:S(2)}) async-start(), calls=%async_computation.2 | async-start | bytes 7077888 | tf_op jit(solution)/shard_map/all_gather | solution.py:122
  7.9 98.2 %all-gather.11.cloned.1.call-start = ((), (), s32[]{:S(2)}) async-start(), calls=%async_computation.3 | async-start | bytes 1474560 | tf_op jit(solution)/shard_map/all_gather | solution.py:150
  9.1 72.6 %copy-start = (f32[160,1536]{1,0:T(8,128)}, f32[160,1536]{1,0:T(8,128)S(1)}, u32[]{:S(2)}) copy-start(f32[160,1536]{1,0:T(8,128)S(1)} %reshape.608) | copy-start | bytes 2949124
  42.6 39.1 %copy-start.27 = (f32[1536]{0:T(1024)}, f32[1536]{0:T(1024)S(1)}, u32[]{:S(2)}) copy-start(f32[1536]{0:T(1024)S(1)} %convert_element_type.151) | copy-start | bytes 18436
  44.1 33.6 %copy-start.30 = (f32[160]{0:T(256)}, f32[160]{0:T(256)S(1)}, u32[]{:S(2)}) copy-start(f32[160]{0:T(256)S(1)} %rsqrt.20) | copy-start | bytes 1924
  45.6 36.7 %copy-start.25 = (f32[160,128]{1,0:T(8,128)}, f32[160,128]{1,0:T(8,128)S(1)}, u32[]{:S(2)}) copy-start(f32[160,128]{1,0:T(8,128)S(1)} %pad_maximum_fusion.4) | copy-start | bytes 245764
  46.4 35.7 %copy-start.24 = (f32[160,128]{1,0:T(8,128)}, f32[160,128]{1,0:T(8,128)S(1)}, u32[]{:S(2)}) copy-start(f32[160,128]{1,0:T(8,128)S(1)} %get-tuple-element.501) | copy-start | bytes 245764
  81.7 24.6 copy-start.11
  83.9 377.3 %all-gather.13.cloned.1.call-start = ((), (), s32[]{:S(2)}) async-start(), calls=%async_computation.4 | async-start | bytes 6553600 | tf_op jit(solution)/shard_map/all_gather | solution.py:175
  106.2 438.7 %all-gather.15.cloned.1.call-start = ((), (), s32[]{:S(2)}) async-start(), calls=%async_computation.5 | async-start | bytes 5308416 | tf_op jit(solution)/shard_map/all_gather | solution.py:123
  106.7 2.0 copy-start.4
  106.7 506.9 %all-gather.19.cloned.1.call-start = ((), (), s32[]{:S(2)}) async-start(), calls=%async_computation.7 | async-start | bytes 30965760 | tf_op jit(solution)/shard_map/all_gather | solution.py:223
  107.3 1054.5 %all-gather.17.cloned.1.call-start = ((), (), s32[]{:S(2)}) async-start(), calls=%async_computation.6 | async-start | bytes 30965760 | tf_op jit(solution)/shard_map/all_gather | solution.py:222
  107.9 1471.5 %all-gather.21.cloned.1.call-start = ((), (), s32[]{:S(2)}) async-start(), calls=%async_computation.8 | async-start | bytes 30965760 | tf_op jit(solution)/shard_map/all_gather | solution.py:232
  108.7 1947.8 %reduce-scatter.5.cloned.1.call-start = ((), (), s32[]{:S(2)}) async-start(), calls=%async_computation.10 | async-start | bytes 30965760 | tf_op jit(solution)/shard_map/reduce_scatter | solution.py:345
  108.7 6.3 collective-permute-start
  122.3 309.6 %collective-permute-start.1 = (bf16[384,8960]{1,0:T(8,128)(2,1)}, bf16[384,8960]{1,0:T(8,128)(2,1)}, u32[]{:S(2)}, u32[]{:S(2)}) collective-permute-start(bf16[384,8960]{1,0:T(8,128)(2,1)} %maximum_select_fusion.3), channel_id=1, source_target_pairs={{0,2},{1,3},{2,0},{3,1},{4,6},{5,7},{6,4},{7,5},{8,10},{9,11},{10,... | collective-permute-start | bytes 20643848 | tf_op jit(solution)/shard_map/ppermute | solution.py:213
  127.9 320.4 %copy-start.12 = (f32[160,2048]{1,0:T(8,128)S(1)}, f32[160,2048]{1,0:T(8,128)}, u32[]{:S(2)}) copy-start(f32[160,2048]{1,0:T(8,128)} %copy-done.11) | copy-start | bytes 3932164
  448.3 1089.9 %collective-permute-start.2 = (bf16[768,8960]{1,0:T(8,128)(2,1)}, bf16[768,8960]{1,0:T(8,128)(2,1)}, u32[]{:S(2)}, u32[]{:S(2)}) collective-permute-start(bf16[768,8960]{1,0:T(8,128)(2,1)} %maximum_select_fusion.2), channel_id=1, source_target_pairs={{0,4},{1,5},{2,6},{3,7},{4,0},{5,1},{6,2},{7,3},{8,12},{9,13},{10,... | collective-permute-start | bytes 41287688 | tf_op jit(solution)/shard_map/ppermute | solution.py:213
  451.7 7.6 copy-start.13
  456.2 5.1 copy-start.29
  544.3 69.4 %copy-start.6 = (bf16[160,1536]{1,0:T(8,128)(2,1)S(1)}, bf16[160,1536]{1,0:T(8,128)(2,1)}, u32[]{:S(2)}) copy-start(bf16[160,1536]{1,0:T(8,128)(2,1)} %reshape.600) | copy-start | bytes 1474564
  544.8 85.9 %copy-start.9 = (bf16[160,1536]{1,0:T(8,128)(2,1)}, bf16[160,1536]{1,0:T(8,128)(2,1)S(1)}, u32[]{:S(2)}) copy-start(bf16[160,1536]{1,0:T(8,128)(2,1)S(1)} %convert_element_type.162) | copy-start | bytes 1474564
  548.7 1063.1 %copy-start.7 = (f32[160,1536]{1,0:T(8,128)}, f32[160,1536]{1,0:T(8,128)S(1)}, u32[]{:S(2)}) copy-start(f32[160,1536]{1,0:T(8,128)S(1)} %get-tuple-element.513) | copy-start | bytes 2949124
  548.9 989.3 %copy-start.14 = (bf16[160,1536]{1,0:T(8,128)(2,1)}, bf16[160,1536]{1,0:T(8,128)(2,1)S(1)}, u32[]{:S(2)}) copy-start(bf16[160,1536]{1,0:T(8,128)(2,1)S(1)} %multiply_convert_fusion.3) | copy-start | bytes 1474564
  1579.3 1106.4 %reduce-scatter.3.cloned.1.call-start = ((), (), s32[]{:S(2)}) async-start(), calls=%async_computation.9 | async-start | bytes 74317824 | tf_op jit(solution)/shard_map/reduce_scatter | solution.py:323
  1612.1 0.9 copy-start.2
  1613.1 5.9 copy-start.16
  1618.2 0.8 copy-start.19
  1632.6 3.9 copy-start.5
  1664.7 3.9 copy-start.5
  1698.0 4.0 copy-start.5
  1731.3 4.1 copy-start.5
  1764.6 4.1 copy-start.5
  1970.2 6.3 copy-start.21
  1974.5 4.4 copy-start.3
  1974.5 4.4 copy-start.10
  1977.5 5.8 copy-start.23
  1978.9 3.6 copy-start.26
  1978.9 3.7 copy-start.17
  1982.5 1.2 copy-start.1
  1982.5 1.2 copy-start.28
  1982.5 1.2 copy-start.31
  1983.7 4.6 copy-start.15
  2056.3 857.5 %all-reduce.14.cloned.1.call-start = ((), (), s32[]{:S(2)}) async-start(), calls=%async_computation.11 | async-start | bytes 23396352 | tf_op jit(solution)/shard_map/psum | solution.py:360
  2685.7 2.1 copy-start.8
  2711.8 2.6 copy-start.32
  2918.5 9.2 copy-start.18
  (2 other events, 1.3 us)
Sparse Core Ops, SparseCore 0:
  9.6 67.9 all-gather.8
  84.0 22.0 all-gather.10
  108.0 60.8 all-gather.12
  170.3 84.2 all-gather.14
  256.1 357.4 all-gather.18
  615.1 546.6 all-gather.16
  1163.4 349.4 all-gather.20
  1579.4 268.8 reduce-scatter.4
  2056.5 629.1 reduce-scatter.2
  2689.3 224.4 all-reduce.13
